TPU v7x, 32 devices: a whole 2x2x4 slice. The times are simulated.
32 devices in a mesh: seq: 8 (over z, y), rep: 4 (over x, core).
Axes of the slice: x: 2, y: 2, z: 4, core: 2. Of those that a mesh axis runs over, the one named last changes fastest.
Arguments:
- inputs: bfloat16 [4, 1024, 1024], P('rep', 'seq'), may hold values from -6 to 6
- weight_t: bfloat16 [3072, 1024], P('seq', 'rep'), may hold values from -0.1875 to 0.1875
- states: float32 [4, 1024, 1024], P('rep', 'seq'), may hold values from -0.9 to 0.9
- doc_ids: int32 [4, 1024], P('rep', 'seq'), may hold values from 0 to 3, never falling along the last dimension, each value on 1 to 512 neighbouring positions
- recur: float32 [3, 1024], replicated, may hold values from -1 to 1
- bias: float32 [3, 1024], replicated, may hold values from -8 to 3, as said below
- out_grad: bfloat16 [4, 1024, 1024], P('rep', 'seq'), may hold values from -6 to 6
Outputs:
- input_grad: bfloat16 [4, 1024, 1024], P('rep', 'seq')
- weight_grad: float32 [3072, 1024], P('seq', 'rep')
- param_grad: float32 [6, 1024], replicated
Inputs may be any that keep to these rules, and one draw needn't show every extreme that they name: `doc_ids`: within each sequence the numbers never fall; every document has 1 to 512 tokens, and some document has exactly 512. `bias`: row 0 lies between -8 and -1, rows 1 and 2 between -3 and 3.
All inputs are finite; a program needn't handle non-finite values.
Results may differ from a plain program's by a relative error of at most 0.0095.
Values may be sent and summed in bfloat16 or wider, within the bound.
A program may use at most 128 MiB of HBM per device.

v0:
```python
import math
import jax
import jax.numpy as jnp
from jax import lax
from jax.sharding import PartitionSpec as P


def shifted(block, axis, distance):
    devices = range(lax.axis_size(axis))
    route = [(i - distance, i) for i in devices if i - distance in devices]
    return lax.ppermute(block, axis, route)


def compose(earlier, later):
    return (later[0] * earlier[0], later[1] + later[0] * earlier[1])


def local(inputs, weight_t, states, doc_ids, recur, bias, out_grad):
    feats = inputs[0]
    hidden_now = states[0]
    ids_float = doc_ids[0].astype(jnp.float32)
    count = feats.shape[0]
    width = hidden_now.shape[1]
    columns = lax.all_gather(weight_t, "rep", axis=1, tiled=True)
    contract_last = (((1,), (1,)), ((), ()))
    full_weight = lax.all_gather(columns, "seq", axis=0, tiled=True)
    preact = lax.dot_general(feats, full_weight, contract_last, preferred_element_type=jnp.float32)
    tail_state, tail_id = shifted((hidden_now[-1:], ids_float[-1:]), "seq", 1)
    first_same = jnp.where(
        (ids_float[0] == tail_id[0]) & (lax.axis_index("seq") > 0), 1.0, 0.0
    ).astype(jnp.float32)
    same = jnp.concatenate(
        [first_same[None], (ids_float[1:] == ids_float[:-1]).astype(jnp.float32)]
    )
    prior = jnp.concatenate([tail_state, hidden_now[:-1]], 0) * same[:, None]
    gate_z = jax.nn.sigmoid(preact[:, :width] + recur[0] * prior + bias[0])
    gate_r = jax.nn.sigmoid(preact[:, width : 2 * width] + recur[1] * prior + bias[1])
    gate_c = jnp.tanh(preact[:, 2 * width :] + recur[2] * gate_r * prior + bias[2])
    jacobian = same[:, None] * (
        1.0
        - gate_z
        + (gate_c - prior) * gate_z * (1.0 - gate_z) * recur[0]
        + gate_z
        * (1.0 - gate_c * gate_c)
        * recur[2]
        * (gate_r + prior * gate_r * (1.0 - gate_r) * recur[1])
    )
    upstream = out_grad[0].astype(jnp.float32)
    jac_rows, up_rows = (
        lax.all_to_all(jacobian.T, "seq", split_axis=0, concat_axis=1, tiled=True),
        lax.all_to_all(upstream.T, "seq", split_axis=0, concat_axis=1, tiled=True),
    )
    factor = jnp.concatenate([jac_rows[:, 1:], jnp.zeros((jac_rows.shape[0], 1), jnp.float32)], 1)
    _, adjoint_rows = lax.associative_scan(compose, (factor, up_rows), reverse=True, axis=1)
    adjoint = lax.all_to_all(adjoint_rows, "seq", split_axis=1, concat_axis=0, tiled=True).T
    grad_z = adjoint * (gate_c - prior) * gate_z * (1.0 - gate_z)
    grad_c = adjoint * gate_z * (1.0 - gate_c * gate_c)
    grad_r = grad_c * recur[2] * prior * gate_r * (1.0 - gate_r)
    grad_pre = jnp.concatenate([grad_z, grad_r, grad_c], 1).astype(jnp.bfloat16)
    input_grad = jnp.dot(grad_pre, full_weight, preferred_element_type=jnp.float32)
    tokens_all = count * inputs.shape[0] * lax.axis_size("seq") * lax.axis_size("rep")
    normal_factor = 1.0 / math.sqrt(tokens_all)
    row_share = lax.psum_scatter(
        lax.dot_general(
            grad_pre, feats, (((0,), (0,)), ((), ())), preferred_element_type=jnp.float32
        ),
        "seq",
        scatter_dimension=0,
        tiled=True,
    )
    weight_grad = (
        lax.psum_scatter(
            row_share.astype(jnp.bfloat16), "rep", scatter_dimension=1, tiled=True
        ).astype(jnp.float32)
        * normal_factor
    )
    stats = jnp.stack(
        [
            grad_z.sum(0),
            grad_r.sum(0),
            grad_c.sum(0),
            (grad_z * prior).sum(0),
            (grad_r * prior).sum(0),
            (grad_c * gate_r * prior).sum(0),
        ]
    )
    param_grad = lax.psum(stats, ("seq", "rep")) * normal_factor
    return (input_grad.astype(jnp.bfloat16)[None], weight_grad, param_grad)


def solution(mesh):
    placed = (
        P("rep", "seq", None),
        P("seq", "rep"),
        P("rep", "seq", None),
        P("rep", "seq"),
        P(),
        P(),
        P("rep", "seq", None),
    )
    return jax.shard_map(
        local,
        mesh=mesh,
        in_specs=placed,
        out_specs=(P("rep", "seq", None), P("seq", "rep"), P()),
        check_vma=False,
    )
```

profile of v0, /device:TPU:0, one launch (start us, length us, event | category | flops | bytes accessed | tf_op | source)
XLA Modules:
  0.0 491.4 jit_solution(18385137196122489823)
XLA Ops:
  7.3 11.8 %all_gather.6 = bf16[384,1024]{1,0:T(8,128)(2,1)} all-gather(bf16[384,256]{1,0:T(8,128)(2,1)} %param.8), channel_id=1, replica_groups=mesh['seq'=8,'rep'=4] {'rep'}, dimensions={1}, use_global_device_ids=true | all-gather | bytes 983040 | tf_op jit(solution)/shard_map/all_gather | solution.py:24
  19.7 4.0 collective-permute-start
  23.7 2.9 collective-permute-start.1
  27.6 4.8 all-to-all-start
  34.1 95.4 %all-gather.2.cloned.1.call-done = bf16[3072,1024]{1,0:T(8,128)(2,1)} async-done(((bf16[384,1024]{1,0:T(8,128)(2,1)}), bf16[3072,1024]{1,0:T(8,128)(2,1)}) %all-gather.2.cloned.1.call-update) | async-done | bytes 6291472 | tf_op jit(solution)/shard_map/all_gather | solution.py:26
  129.5 5.0 %fusion.21 = f32[128,3072]{1,0:T(8,128)S(1)} fusion(bf16[3072,1024]{1,0:T(8,128)(2,1)} %all-gather.2.cloned.1.call-done, bf16[1,128,1024]{2,1,0:T(8,128)(2,1)S(1)} %copy-done), kind=kOutput, calls=%fused_computation.40 | convolution fusion | flops 805306368 | bytes 8126464 | tf_op jit(solution)/shard_map/dot_general | solution.py:27
  134.5 1.6 copy_bitcast_fusion
  136.1 4.2 all-to-all-start.1
  140.5 1.4 slice.317
  143.2 1.9 slice.318
  145.1 1.3 slice.342
  147.8 5.9 %all-to-all-done.1 = f32[8,128,128]{1,2,0:T(8,128)} async-done(((f32[8,128,128]{1,2,0:T(8,128)}), f32[8,128,128]{1,2,0:T(8,128)}, u32[]{:S(2)}, u32[]{:S(2)}) %all-to-all-start.1) | async-done | bytes 524320 | tf_op jit(solution)/shard_map/all_to_all | solution.py:50
  154.8 1.4 slice.339
  156.2 1.4 slice.343
  158.0 2.9 slice.344
  184.8 1.9 slice.340
  201.4 3.4 rev.2
  204.9 17.3 %all_to_all.63 = f32[128,8,128]{0,2,1:T(8,128)S(1)} all-to-all(f32[128,8,128]{0,2,1:T(8,128)S(1)} %bitcast.86), channel_id=1, replica_groups=mesh['seq'=8,'rep'=4] {'seq'}, dimensions={1} | all-to-all | bytes 1048576 | tf_op jit(solution)/shard_map/all_to_all | solution.py:55
  223.1 6.3 %fusion.18 = f32[3072,1024]{1,0:T(8,128)} fusion(bf16[128,1024]{1,0:T(8,128)(2,1)S(1)} %get-tuple-element.11, bf16[128,1024]{1,0:T(8,128)(2,1)S(1)} %get-tuple-element.10, bf16[128,1024]{1,0:T(8,128)(2,1)S(1)} %get-tuple-element.9, bf16[1,128,1024]{2,1,0:T(8,128)(2,1)S(1)} %copy-done), kind=kOutput, calls=%fused_computation.34 | convolution fusion | flops 807665664 | bytes 13631488 | tf_op jit(solution)/shard_map/dot_general | solution.py:64
  229.6 206.6 %reduce-scatter.3.cloned.1.call-done = f32[384,1024]{1,0:T(8,128)} async-done(((f32[3072,1024]{1,0:T(8,128)}), f32[384,1024]{1,0:T(8,128)}) %reduce-scatter.3.cloned.1.call-update) | async-done | bytes 1572880 | tf_op jit(solution)/shard_map/reduce_scatter | solution.py:63
  436.1 2.4 convert_element_type.29
  438.6 39.5 %psum.7 = f32[6,1024]{1,0:T(8,128)S(1)} all-reduce(f32[6,1024]{1,0:T(8,128)S(1)} %stack.27), channel_id=1, replica_groups=mesh['seq'=8,'rep'=4] {'seq','rep'}, use_global_device_ids=true, to_apply=%region_8.9 | all-reduce | flops 6144 | bytes 49152 | tf_op jit(solution)/shard_map/psum | solution.py:87
  478.7 4.5 fusion
  483.2 1.7 convert_multiply_fusion
  (191 shorter events, 46.3 us)
Async XLA Ops:
  7.2 122.3 %copy-start = (bf16[1,128,1024]{2,1,0:T(8,128)(2,1)S(1)}, bf16[1,128,1024]{2,1,0:T(8,128)(2,1)}, u32[]{:S(2)}) copy-start(bf16[1,128,1024]{2,1,0:T(8,128)(2,1)} %param.7) | copy-start | bytes 786436
  7.2 19.4 %copy-start.2 = (bf16[1,128,1024]{2,1,0:T(8,128)(2,1)S(1)}, bf16[1,128,1024]{2,1,0:T(8,128)(2,1)}, u32[]{:S(2)}) copy-start(bf16[1,128,1024]{2,1,0:T(8,128)(2,1)} %param.13) | copy-start | bytes 786436
  7.2 122.2 %all-gather.2.cloned.1.call-start = ((), (), s32[]{:S(2)}) async-start(), calls=%async_computation.5 | async-start | bytes 7077888 | tf_op jit(solution)/shard_map/all_gather | solution.py:26
  19.7 13.0 %collective-permute-start = (f32[1]{0:T(128)}, f32[1]{0:T(128)}, u32[]{:S(2)}, u32[]{:S(2)}) collective-permute-start(f32[1]{0:T(128)} %bitcast.6), channel_id=1, source_target_pairs={{0,4},{4,8},{8,12},{12,16},{16,20},{20,24},{24,28},{1,5},{5,9},{9,... | collective-permute-start | bytes 20 | tf_op jit(solution)/shard_map/ppermute | solution.py:11
  23.7 110.7 %collective-permute-start.1 = (f32[1,1024]{1,0:T(1,128)S(1)}, f32[1,1024]{1,0:T(1,128)S(1)}, u32[]{:S(2)}, u32[]{:S(2)}) collective-permute-start(f32[1,1024]{1,0:T(1,128)S(1)} %slice_bitcast_fusion.1), channel_id=1, source_target_pairs={{0,4},{4,8},{8,12},{12,16},{16,20},{20,24},{24,28},{1,5},{5,9},{9,... | collective-permute-start | bytes 12296 | tf_op jit(solution)/shard_map/ppermute | solution.py:11
  27.6 108.5 %all-to-all-start = ((f32[8,128,128]{2,1,0:T(8,128)}), f32[8,128,128]{2,1,0:T(8,128)S(1)}, u32[]{:S(2)}, u32[]{:S(2)}) async-start(f32[8,128,128]{2,1,0:T(8,128)} %bitcast.2), calls=%async_computation | async-start | bytes 1048576 | tf_op jit(solution)/shard_map/all_to_all | solution.py:51
  32.5 101.9 %copy-start.3 = (f32[1,1024]{1,0:T(1,128)}, f32[1,1024]{1,0:T(1,128)S(1)}, u32[]{:S(2)}) copy-start(f32[1,1024]{1,0:T(1,128)S(1)} %get-tuple-element.25) | copy-start | bytes 12292
  32.5 101.9 %copy-start.5 = (f32[1,1024]{1,0:T(1,128)}, f32[1,1024]{1,0:T(1,128)S(1)}, u32[]{:S(2)}) copy-start(f32[1,1024]{1,0:T(1,128)S(1)} %get-tuple-element.26) | copy-start | bytes 12292
  32.5 101.9 %copy-start.7 = (f32[1,1024]{1,0:T(1,128)}, f32[1,1024]{1,0:T(1,128)S(1)}, u32[]{:S(2)}) copy-start(f32[1,1024]{1,0:T(1,128)S(1)} %get-tuple-element.27) | copy-start | bytes 12292
  32.6 101.9 %copy-start.9 = (f32[1,1024]{1,0:T(1,128)}, f32[1,1024]{1,0:T(1,128)S(1)}, u32[]{:S(2)}) copy-start(f32[1,1024]{1,0:T(1,128)S(1)} %get-tuple-element.22) | copy-start | bytes 12292
  32.6 101.9 %copy-start.11 = (f32[1,1024]{1,0:T(1,128)}, f32[1,1024]{1,0:T(1,128)S(1)}, u32[]{:S(2)}) copy-start(f32[1,1024]{1,0:T(1,128)S(1)} %get-tuple-element.23) | copy-start | bytes 12292
  32.6 101.9 %copy-start.13 = (f32[1,1024]{1,0:T(1,128)}, f32[1,1024]{1,0:T(1,128)S(1)}, u32[]{:S(2)}) copy-start(f32[1,1024]{1,0:T(1,128)S(1)} %get-tuple-element.24) | copy-start | bytes 12292
  34.1 100.5 %copy-start.19 = (f32[128]{0:T(128)}, f32[128]{0:T(128)S(1)}, u32[]{:S(2)}) copy-start(f32[128]{0:T(128)S(1)} %pad_maximum_fusion.12) | copy-start | bytes 1540
  136.1 17.6 %all-to-all-start.1 = ((f32[8,128,128]{1,2,0:T(8,128)}), f32[8,128,128]{1,2,0:T(8,128)}, u32[]{:S(2)}, u32[]{:S(2)}) async-start(f32[8,128,128]{1,2,0:T(8,128)} %copy_bitcast_fusion), calls=%async_computation.1 | async-start | bytes 1048576 | tf_op jit(solution)/shard_map/all_to_all | solution.py:50
  140.3 295.8 %reduce-scatter.3.cloned.1.call-start = ((), (), s32[]{:S(2)}) async-start(), calls=%async_computation.6 | async-start | bytes 14155776 | tf_op jit(solution)/shard_map/reduce_scatter | solution.py:63
  200.5 21.6 %copy-start.4 = (f32[1,1024]{1,0:T(1,128)S(1)}, f32[1,1024]{1,0:T(1,128)}, u32[]{:S(2)}) copy-start(f32[1,1024]{1,0:T(1,128)} %copy-done.3) | copy-start | bytes 12292
  200.5 21.6 %copy-start.6 = (f32[1,1024]{1,0:T(1,128)S(1)}, f32[1,1024]{1,0:T(1,128)}, u32[]{:S(2)}) copy-start(f32[1,1024]{1,0:T(1,128)} %copy-done.5) | copy-start | bytes 12292
  200.5 21.6 %copy-start.8 = (f32[1,1024]{1,0:T(1,128)S(1)}, f32[1,1024]{1,0:T(1,128)}, u32[]{:S(2)}) copy-start(f32[1,1024]{1,0:T(1,128)} %copy-done.7) | copy-start | bytes 12292
  200.5 21.6 %copy-start.10 = (f32[1,1024]{1,0:T(1,128)S(1)}, f32[1,1024]{1,0:T(1,128)}, u32[]{:S(2)}) copy-start(f32[1,1024]{1,0:T(1,128)} %copy-done.9) | copy-start | bytes 12292
  200.5 21.6 %copy-start.12 = (f32[1,1024]{1,0:T(1,128)S(1)}, f32[1,1024]{1,0:T(1,128)}, u32[]{:S(2)}) copy-start(f32[1,1024]{1,0:T(1,128)} %copy-done.11) | copy-start | bytes 12292
  200.5 21.6 %copy-start.14 = (f32[1,1024]{1,0:T(1,128)S(1)}, f32[1,1024]{1,0:T(1,128)}, u32[]{:S(2)}) copy-start(f32[1,1024]{1,0:T(1,128)} %copy-done.13) | copy-start | bytes 12292
  200.5 21.6 %copy-start.16 = (f32[1,1024]{1,0:T(1,128)S(1)}, f32[1,1024]{1,0:T(1,128)}, u32[]{:S(2)}) copy-start(f32[1,1024]{1,0:T(1,128)} %copy-done.15) | copy-start | bytes 12292
  200.6 21.6 %copy-start.20 = (f32[128]{0:T(128)S(1)}, f32[128]{0:T(128)}, u32[]{:S(2)}) copy-start(f32[128]{0:T(128)} %copy-done.19) | copy-start | bytes 1540
  229.5 253.7 %reduce-scatter.5.cloned.1.call-start = ((), (), s32[]{:S(2)}) async-start(), calls=%async_computation.7 | async-start | bytes 983040 | tf_op jit(solution)/shard_map/reduce_scatter | solution.py:72
  (8 other events, 76.0 us)
Sparse Core Ops, SparseCore 0:
  19.2 110.1 all-gather.1
  229.6 206.4 reduce-scatter.2
  438.7 22.3 reduce-scatter.4
where the time goes:
time: 493 us; the launch traced here: 491 us
  waiting for transfers between devices  308 us (62%)
  blocking collectives  68.6 us (14%)
  local copies, waits for them, and re-layouts  42.2 us (9%)
  other arithmetic  25.3 us (5%)
  starting transfers between devices  16 us (3%)
  matrix products  15.8 us (3%)
  between operations  15.7 us (3%)
    reduce_scatter x1, waiting for transfers between devices, local(): lax.psum_scatter(lax.dot_general(grad_pre, feats, (((0,), (0,)), ((), ())...  207 us
    all_gather x1, waiting for transfers between devices, local(): full_weight = lax.all_gather(columns, 'seq', axis=0, tiled=True)  95.4 us
    psum x1, blocking collectives, local(): param_grad = lax.psum(stats, ('seq', 'rep')) * normal_factor  39.5 us
    slice x66, local copies, waits for them, and re-layouts, local(): lax.associative_scan(compose, (factor, up_rows), reverse=True, axis=1)  33.1 us
    all_to_all x1, blocking collectives, local(): lax.all_to_all(adjoint_rows, 'seq', split_axis=1, concat_axis=0, tiled=True)  17.3 us
    all_gather x1, blocking collectives, local(): columns = lax.all_gather(weight_t, 'rep', axis=1, tiled=True)  11.8 us
  transfers between devices with their start and end apart: 7, of which 3 were waited for; matrix products, arithmetic and copies ran while one was open for 4% of the time, Pallas kernels for 0%

commit v1 on v0

--- a/solution.py
+++ b/solution.py
@@ -23,7 +23,9 @@
     width = hidden_now.shape[1]
     columns = lax.all_gather(weight_t, "rep", axis=1, tiled=True)
     contract_last = (((1,), (1,)), ((), ()))
-    full_weight = lax.all_gather(columns, "seq", axis=0, tiled=True)
+    full_weight = jnp.concatenate(
+        lax.all_to_all(jnp.stack([columns] * lax.axis_size("seq")), "seq", 0, 0), axis=0
+    )
     preact = lax.dot_general(feats, full_weight, contract_last, preferred_element_type=jnp.float32)
     tail_state, tail_id = shifted((hidden_now[-1:], ids_float[-1:]), "seq", 1)
     first_same = jnp.where(

time: 493 us -> 543 us (1.10)
  waiting for transfers between devices: 308 us -> 349 us
    all_to_all x0 -> x1, waiting for transfers between devices: none -> 130 us  [local(): lax.all_to_all(jnp.stack([columns] * lax.axis_size('seq')), 'seq', 0, 0)]
    all_gather x1 -> x0, waiting for transfers between devices: 95.4 us -> none  [local(): full_weight = lax.all_gather(columns, 'seq', axis=0, tiled=True)]
    all_to_all x1, waiting for transfers between devices: 0.01 us -> 6.55 us  [local(): lax.all_to_all(upstream.T, 'seq', split_axis=0, concat_axis=1, tiled=True)]
    all_to_all x0 -> x1, starting transfers between devices: none -> 5.98 us  [local(): lax.all_to_all(jnp.stack([columns] * lax.axis_size('seq')), 'seq', 0, 0)]
  transfers between devices with their start and end apart: 7 -> 7, of which waited for: 3 -> 4; matrix products, arithmetic and copies ran while one was open for 4% -> 4% of each run, Pallas kernels for 0% -> 0%
where the time goes in v1:
time: 543 us; the launch traced here: 541 us
  waiting for transfers between devices  349 us (64%)
  blocking collectives  67.9 us (13%)
  local copies, waits for them, and re-layouts  45.8 us (8%)
  other arithmetic  25.4 us (5%)
  starting transfers between devices  21.2 us (4%)
  between operations  16 us (3%)
  matrix products  15.8 us (3%)
    reduce_scatter x1, waiting for transfers between devices, local(): lax.psum_scatter(lax.dot_general(grad_pre, feats, (((0,), (0,)), ((), ())...  206 us
    all_to_all x1, waiting for transfers between devices, local(): lax.all_to_all(jnp.stack([columns] * lax.axis_size('seq')), 'seq', 0, 0)  130 us
    psum x1, blocking collectives, local(): param_grad = lax.psum(stats, ('seq', 'rep')) * normal_factor  39.4 us
    slice x66, local copies, waits for them, and re-layouts, local(): lax.associative_scan(compose, (factor, up_rows), reverse=True, axis=1)  33.3 us
    all_to_all x1, blocking collectives, local(): lax.all_to_all(adjoint_rows, 'seq', split_axis=1, concat_axis=0, tiled=True)  18 us
  transfers between devices with their start and end apart: 7, of which 4 were waited for; matrix products, arithmetic and copies ran while one was open for 4% of the time, Pallas kernels for 0%

profile of v1, /device:TPU:0, one launch (start us, length us, event | category | flops | bytes accessed | tf_op | source)
XLA Modules:
  0.0 541.3 jit_solution(16782280125979112429)
XLA Ops:
  7.2 10.4 %all_gather.3 = bf16[384,1024]{1,0:T(8,128)(2,1)S(1)} all-gather(bf16[384,256]{1,0:T(8,128)(2,1)} %param.8), channel_id=1, replica_groups=mesh['seq'=8,'rep'=4] {'rep'}, dimensions={1}, use_global_device_ids=true | all-gather | bytes 983040 | tf_op jit(solution)/shard_map/all_gather | solution.py:24
  17.6 3.5 stack.32
  21.1 6.0 %all-to-all-start.1 = ((bf16[8,384,1024]{2,1,0:T(8,128)(2,1)}), bf16[8,384,1024]{2,1,0:T(8,128)(2,1)}, u32[]{:S(2)}, u32[]{:S(2)}) async-start(bf16[8,384,1024]{2,1,0:T(8,128)(2,1)} %stack.32), calls=%async_computation.1 | async-start | bytes 12582912 | tf_op jit(solution)/shard_map/all_to_all | solution.py:27
  27.7 4.5 collective-permute-start
  32.1 2.8 collective-permute-start.1
  36.2 129.6 %all-to-all-done.1 = bf16[8,384,1024]{2,1,0:T(8,128)(2,1)} async-done(((bf16[8,384,1024]{2,1,0:T(8,128)(2,1)}), bf16[8,384,1024]{2,1,0:T(8,128)(2,1)}, u32[]{:S(2)}, u32[]{:S(2)}) %all-to-all-start.1) | async-done | bytes 6291488 | tf_op jit(solution)/shard_map/all_to_all | solution.py:27
  165.8 3.7 all-to-all-start
  170.9 5.0 fusion.21
  176.0 1.6 copy_bitcast_fusion
  177.6 6.5 %all-to-all-done = f32[8,128,128]{2,1,0:T(8,128)S(1)} async-done(((f32[8,128,128]{2,1,0:T(8,128)}), f32[8,128,128]{2,1,0:T(8,128)S(1)}, u32[]{:S(2)}, u32[]{:S(2)}) %all-to-all-start) | async-done | bytes 524320 | tf_op jit(solution)/shard_map/all_to_all | solution.py:53
  184.1 4.1 all-to-all-start.2
  188.5 1.4 slice.317
  191.2 1.9 slice.318
  195.7 6.8 %all-to-all-done.2 = f32[8,128,128]{1,2,0:T(8,128)} async-done(((f32[8,128,128]{1,2,0:T(8,128)}), f32[8,128,128]{1,2,0:T(8,128)}, u32[]{:S(2)}, u32[]{:S(2)}) %all-to-all-start.2) | async-done | bytes 524320 | tf_op jit(solution)/shard_map/all_to_all | solution.py:52
  206.8 2.9 slice.344
  233.8 1.9 slice.340
  250.6 3.4 rev.2
  254.1 18.0 %all_to_all.68 = f32[128,8,128]{0,2,1:T(8,128)S(1)} all-to-all(f32[128,8,128]{0,2,1:T(8,128)S(1)} %bitcast.87), channel_id=1, replica_groups=mesh['seq'=8,'rep'=4] {'seq'}, dimensions={1} | all-to-all | bytes 1048576 | tf_op jit(solution)/shard_map/all_to_all | solution.py:57
  273.1 6.4 %fusion.18 = f32[3072,1024]{1,0:T(8,128)} fusion(bf16[128,1024]{1,0:T(8,128)(2,1)S(1)} %get-tuple-element.11, bf16[128,1024]{1,0:T(8,128)(2,1)S(1)} %get-tuple-element.10, bf16[128,1024]{1,0:T(8,128)(2,1)S(1)} %get-tuple-element.9, bf16[1,128,1024]{2,1,0:T(8,128)(2,1)S(1)} %copy-done), kind=kOutput, calls=%fused_computation.34 | convolution fusion | flops 807665664 | bytes 13631488 | tf_op jit(solution)/shard_map/dot_general | solution.py:66
  279.5 206.2 %reduce-scatter.3.cloned.1.call-done = f32[384,1024]{1,0:T(8,128)} async-done(((f32[3072,1024]{1,0:T(8,128)}), f32[384,1024]{1,0:T(8,128)}) %reduce-scatter.3.cloned.1.call-update) | async-done | bytes 1572880 | tf_op jit(solution)/shard_map/reduce_scatter | solution.py:65
  485.7 2.4 convert_element_type.29
  488.2 39.4 %psum.7 = f32[6,1024]{1,0:T(8,128)S(1)} all-reduce(f32[6,1024]{1,0:T(8,128)S(1)} %stack.39), channel_id=1, replica_groups=mesh['seq'=8,'rep'=4] {'seq','rep'}, use_global_device_ids=true, to_apply=%region_8.9 | all-reduce | flops 6144 | bytes 49152 | tf_op jit(solution)/shard_map/psum | solution.py:89
  528.3 4.5 fusion
  532.8 1.7 convert_multiply_fusion
  (191 shorter events, 50.7 us)
Async XLA Ops:
  7.2 163.8 %copy-start = (bf16[1,128,1024]{2,1,0:T(8,128)(2,1)S(1)}, bf16[1,128,1024]{2,1,0:T(8,128)(2,1)}, u32[]{:S(2)}) copy-start(bf16[1,128,1024]{2,1,0:T(8,128)(2,1)} %param.7) | copy-start | bytes 786436
  21.1 14.1 %copy-start.17 = (f32[3,1024]{1,0:T(4,128)S(1)}, f32[3,1024]{1,0:T(4,128)}, u32[]{:S(2)}) copy-start(f32[3,1024]{1,0:T(4,128)} %param.12) | copy-start | bytes 36868
  21.1 14.1 %copy-start.18 = (f32[3,1024]{1,0:T(4,128)S(1)}, f32[3,1024]{1,0:T(4,128)}, u32[]{:S(2)}) copy-start(f32[3,1024]{1,0:T(4,128)} %param.11) | copy-start | bytes 36868
  21.1 144.7 %all-to-all-start.1 = ((bf16[8,384,1024]{2,1,0:T(8,128)(2,1)}), bf16[8,384,1024]{2,1,0:T(8,128)(2,1)}, u32[]{:S(2)}, u32[]{:S(2)}) async-start(bf16[8,384,1024]{2,1,0:T(8,128)(2,1)} %stack.32), calls=%async_computation.1 | async-start | bytes 12582912 | tf_op jit(solution)/shard_map/all_to_all | solution.py:27
  27.7 141.9 %collective-permute-start = (f32[1]{0:T(128)}, f32[1]{0:T(128)}, u32[]{:S(2)}, u32[]{:S(2)}) collective-permute-start(f32[1]{0:T(128)} %bitcast.6), channel_id=1, source_target_pairs={{0,4},{4,8},{8,12},{12,16},{16,20},{20,24},{24,28},{1,5},{5,9},{9,... | collective-permute-start | bytes 20 | tf_op jit(solution)/shard_map/ppermute | solution.py:11
  32.1 143.7 %collective-permute-start.1 = (f32[1,1024]{1,0:T(1,128)S(1)}, f32[1,1024]{1,0:T(1,128)S(1)}, u32[]{:S(2)}, u32[]{:S(2)}) collective-permute-start(f32[1,1024]{1,0:T(1,128)S(1)} %slice_bitcast_fusion.1), channel_id=1, source_target_pairs={{0,4},{4,8},{8,12},{12,16},{16,20},{20,24},{24,28},{1,5},{5,9},{9,... | collective-permute-start | bytes 12296 | tf_op jit(solution)/shard_map/ppermute | solution.py:11
  35.2 140.7 %copy-start.3 = (f32[1,1024]{1,0:T(1,128)}, f32[1,1024]{1,0:T(1,128)S(1)}, u32[]{:S(2)}) copy-start(f32[1,1024]{1,0:T(1,128)S(1)} %get-tuple-element.25) | copy-start | bytes 12292
  35.2 140.7 %copy-start.5 = (f32[1,1024]{1,0:T(1,128)}, f32[1,1024]{1,0:T(1,128)S(1)}, u32[]{:S(2)}) copy-start(f32[1,1024]{1,0:T(1,128)S(1)} %get-tuple-element.26) | copy-start | bytes 12292
  35.2 140.7 %copy-start.7 = (f32[1,1024]{1,0:T(1,128)}, f32[1,1024]{1,0:T(1,128)S(1)}, u32[]{:S(2)}) copy-start(f32[1,1024]{1,0:T(1,128)S(1)} %get-tuple-element.27) | copy-start | bytes 12292
  35.2 140.7 %copy-start.9 = (f32[1,1024]{1,0:T(1,128)}, f32[1,1024]{1,0:T(1,128)S(1)}, u32[]{:S(2)}) copy-start(f32[1,1024]{1,0:T(1,128)S(1)} %get-tuple-element.22) | copy-start | bytes 12292
  35.3 140.7 %copy-start.11 = (f32[1,1024]{1,0:T(1,128)}, f32[1,1024]{1,0:T(1,128)S(1)}, u32[]{:S(2)}) copy-start(f32[1,1024]{1,0:T(1,128)S(1)} %get-tuple-element.23) | copy-start | bytes 12292
  35.3 140.7 %copy-start.13 = (f32[1,1024]{1,0:T(1,128)}, f32[1,1024]{1,0:T(1,128)S(1)}, u32[]{:S(2)}) copy-start(f32[1,1024]{1,0:T(1,128)S(1)} %get-tuple-element.24) | copy-start | bytes 12292
  165.8 18.3 %all-to-all-start = ((f32[8,128,128]{2,1,0:T(8,128)}), f32[8,128,128]{2,1,0:T(8,128)S(1)}, u32[]{:S(2)}, u32[]{:S(2)}) async-start(f32[8,128,128]{2,1,0:T(8,128)} %bitcast.2), calls=%async_computation | async-start | bytes 1048576 | tf_op jit(solution)/shard_map/all_to_all | solution.py:53
  184.1 18.4 %all-to-all-start.2 = ((f32[8,128,128]{1,2,0:T(8,128)}), f32[8,128,128]{1,2,0:T(8,128)}, u32[]{:S(2)}, u32[]{:S(2)}) async-start(f32[8,128,128]{1,2,0:T(8,128)} %copy_bitcast_fusion), calls=%async_computation.2 | async-start | bytes 1048576 | tf_op jit(solution)/shard_map/all_to_all | solution.py:52
  188.3 297.5 %reduce-scatter.3.cloned.1.call-start = ((), (), s32[]{:S(2)}) async-start(), calls=%async_computation.6 | async-start | bytes 14155776 | tf_op jit(solution)/shard_map/reduce_scatter | solution.py:65
  249.7 22.4 %copy-start.4 = (f32[1,1024]{1,0:T(1,128)S(1)}, f32[1,1024]{1,0:T(1,128)}, u32[]{:S(2)}) copy-start(f32[1,1024]{1,0:T(1,128)} %copy-done.3) | copy-start | bytes 12292
  249.7 22.4 %copy-start.6 = (f32[1,1024]{1,0:T(1,128)S(1)}, f32[1,1024]{1,0:T(1,128)}, u32[]{:S(2)}) copy-start(f32[1,1024]{1,0:T(1,128)} %copy-done.5) | copy-start | bytes 12292
  249.7 22.4 %copy-start.8 = (f32[1,1024]{1,0:T(1,128)S(1)}, f32[1,1024]{1,0:T(1,128)}, u32[]{:S(2)}) copy-start(f32[1,1024]{1,0:T(1,128)} %copy-done.7) | copy-start | bytes 12292
  249.7 22.4 %copy-start.10 = (f32[1,1024]{1,0:T(1,128)S(1)}, f32[1,1024]{1,0:T(1,128)}, u32[]{:S(2)}) copy-start(f32[1,1024]{1,0:T(1,128)} %copy-done.9) | copy-start | bytes 12292
  249.7 22.4 %copy-start.12 = (f32[1,1024]{1,0:T(1,128)S(1)}, f32[1,1024]{1,0:T(1,128)}, u32[]{:S(2)}) copy-start(f32[1,1024]{1,0:T(1,128)} %copy-done.11) | copy-start | bytes 12292
  249.7 22.4 %copy-start.14 = (f32[1,1024]{1,0:T(1,128)S(1)}, f32[1,1024]{1,0:T(1,128)}, u32[]{:S(2)}) copy-start(f32[1,1024]{1,0:T(1,128)} %copy-done.13) | copy-start | bytes 12292
  249.8 22.4 %copy-start.16 = (f32[1,1024]{1,0:T(1,128)S(1)}, f32[1,1024]{1,0:T(1,128)}, u32[]{:S(2)}) copy-start(f32[1,1024]{1,0:T(1,128)} %copy-done.15) | copy-start | bytes 12292
  249.8 22.4 %copy-start.20 = (f32[128]{0:T(128)S(1)}, f32[128]{0:T(128)}, u32[]{:S(2)}) copy-start(f32[128]{0:T(128)} %copy-done.19) | copy-start | bytes 1540
  279.5 253.3 %reduce-scatter.5.cloned.1.call-start = ((), (), s32[]{:S(2)}) async-start(), calls=%async_computation.7 | async-start | bytes 983040 | tf_op jit(solution)/shard_map/reduce_scatter | solution.py:74
  (8 other events, 63.7 us)
Sparse Core Ops, SparseCore 0:
  279.6 206.0 reduce-scatter.2
  488.3 22.2 reduce-scatter.4
